TPU v7x, 128 devices: a whole 4x4x4 slice. The times are simulated.
128 devices in a mesh: section: 4 (over y), wide: 8 (over z, x_hi), narrow: 4 (over x_lo, core).
Axes of the slice: x: 4 (x_hi: 2, x_lo: 2; x = x_hi * 2 + x_lo), y: 4, z: 4, core: 2. Of those that a mesh axis runs over, the one named last changes fastest.
Arguments:
- normed_inputs: bfloat16 [4, 4, 4, 768, 4096], P('section', 'narrow', None, 'wide'), may hold values from -160 to 160
- value_cotangent: bfloat16 [4, 4, 4, 768, 1024], P('section', 'narrow', None, 'wide'), may hold values from -6 to 6
- expert_hidden: bfloat16 [4, 4, 4, 256, 7168], P('section', 'narrow', None, None, 'wide'), may hold values from -40 to 40
- expert_cotangent: bfloat16 [4, 4, 4, 256, 4096], P('section', 'narrow', None, 'wide'), may hold values from -110 to 110
- slot_gate: bfloat16 [4, 4, 4, 256], P('section', 'narrow', None, 'wide'), may hold values from 0.25 to 1
- slot_count: int32 [4, 4, 4], P('section', 'narrow'), may hold values from 129 to 256, as said below
- expert_weight: bfloat16 [4, 7168, 4096], P('section', 'wide', 'narrow'), may hold values from -0.0625 to 0.0625
- expert_moment: float32 [4, 7168, 4096], P('section', 'wide', 'narrow'), may hold values from -6 to 6
- value_weight: bfloat16 [4, 4096, 1024], P('section', ('wide', 'narrow')), may hold values from -0.09375 to 0.09375
- value_moment: float32 [4, 4096, 1024], P('section', ('wide', 'narrow')), may hold values from -6 to 6
Outputs:
- expert_weight_next: bfloat16 [4, 7168, 4096], P('section', 'wide', 'narrow')
- expert_moment_next: float32 [4, 7168, 4096], P('section', 'wide', 'narrow')
- value_weight_next: bfloat16 [4, 4096, 1024], P('section', ('wide', 'narrow'))
- value_moment_next: float32 [4, 4096, 1024], P('section', ('wide', 'narrow'))
Inputs may be any that keep to these rules, and one draw needn't show every extreme that they name: The live slots of a micro-batch are slots 0 to slot_count - 1; in every layer and replica some micro-batch fills all 256 slots.
All inputs are finite; a program needn't handle non-finite values.
Results may differ from a plain program's by a relative error of at most 0.014.
Values may be sent and summed in bfloat16 or wider, within the bound.
A program may use at most 128 MiB of HBM per device.

v0:
```python
import math
import jax
import jax.numpy as jnp
from jax import lax
from jax.sharding import Mesh
from jax.sharding import PartitionSpec as P

D = 4096
FF = 7168
KV = 1024
WIDE = ("wide_0", "wide_1")
NARROW = ("narrow_0", "narrow_1")
WIDE_NARROW = ("wide_0", "wide_1", "narrow_0", "narrow_1")
SECTION_WIDE_NARROW = ("section", "wide_0", "wide_1", "narrow_0", "narrow_1")
MOMENTUM_DECAY = 0.9
STEP_RATE = 0.01


def over_axes(shard, axes):
    for axis in axes:
        shard = lax.psum(shard, axis)
    return shard


def on_device(
    normed_inputs,
    value_cotangent,
    expert_hidden,
    expert_cotangent,
    slot_gate,
    slot_count,
    expert_weight,
    expert_moment,
    value_weight,
    value_moment,
):
    input_rows = normed_inputs[0, 0].reshape(-1, normed_inputs.shape[-1])
    value_cot_rows = value_cotangent[0, 0].reshape(-1, value_cotangent.shape[-1])
    hidden_local = expert_hidden[0, 0]
    cotangent = expert_cotangent[0, 0]
    gate_local = slot_gate[0, 0]
    live_count = slot_count[0, 0]
    cot_piece = lax.all_gather(cotangent, WIDE, axis=1, tiled=True)
    gate_piece = lax.all_gather(gate_local, WIDE, axis=1, tiled=True)
    length = cot_piece.shape[1]
    positions = jnp.arange(length, dtype=jnp.int32)
    live = positions[None, :] < live_count[:, None]
    coefficient = jnp.where(
        live, gate_piece.astype(jnp.float32), jnp.zeros(gate_piece.shape, jnp.float32)
    )
    scaled = (coefficient[:, :, None] * cot_piece.astype(jnp.float32)).astype(jnp.bfloat16)
    summed = lax.dot_general(
        hidden_local, scaled, (((0, 1), (0, 1)), ((), ())), preferred_element_type=jnp.float32
    )
    expert_grad = lax.psum_scatter(
        summed.astype(jnp.bfloat16), NARROW, scatter_dimension=1, tiled=True
    ).astype(jnp.float32)
    value_grad = lax.psum_scatter(
        lax.dot_general(
            input_rows, value_cot_rows, (((0,), (0,)), ((), ())), preferred_element_type=jnp.float32
        ).astype(jnp.bfloat16),
        WIDE_NARROW,
        scatter_dimension=0,
        tiled=True,
    ).astype(jnp.float32)
    squares = jnp.sum(expert_grad * expert_grad) + jnp.sum(value_grad * value_grad)
    overall = over_axes(squares, SECTION_WIDE_NARROW)
    entry_count = lax.axis_size("section") * (FF * D + D * KV)
    factor = jnp.minimum(1.0, math.sqrt(entry_count) / jnp.sqrt(overall + 1e-06))
    expert_next = MOMENTUM_DECAY * expert_moment[0] + factor * expert_grad
    value_next = MOMENTUM_DECAY * value_moment[0] + factor * value_grad
    expert_weight_next = (expert_weight[0].astype(jnp.float32) - STEP_RATE * expert_next).astype(
        jnp.bfloat16
    )
    value_weight_next = (value_weight[0].astype(jnp.float32) - STEP_RATE * value_next).astype(
        jnp.bfloat16
    )
    return (expert_weight_next[None], expert_next[None], value_weight_next[None], value_next[None])


def solution(mesh):
    finer = Mesh(
        mesh.devices.reshape(mesh.shape["section"], 4, 2, 2, 2),
        ("section", "wide_0", "wide_1", "narrow_0", "narrow_1"),
    )
    in_specs = (
        P("section", NARROW, None, WIDE, None),
        P("section", NARROW, None, WIDE, None),
        P("section", NARROW, None, None, WIDE),
        P("section", NARROW, None, WIDE, None),
        P("section", NARROW, None, WIDE),
        P("section", NARROW, None),
        P("section", WIDE, NARROW),
        P("section", WIDE, NARROW),
        P("section", WIDE_NARROW, None),
        P("section", WIDE_NARROW, None),
    )
    out_specs = (
        P("section", WIDE, NARROW),
        P("section", WIDE, NARROW),
        P("section", WIDE_NARROW, None),
        P("section", WIDE_NARROW, None),
    )
    return jax.shard_map(
        on_device, mesh=finer, in_specs=in_specs, out_specs=out_specs, check_vma=False
    )
```

profile of v0, /device:TPU:1, one launch (start us, length us, event | category | flops | bytes accessed | tf_op | source)
XLA Modules:
  0.0 304.2 jit_solution(16088000934408733016)
XLA Ops:
  8.0 0.0 copy-start
  8.0 0.0 all-gather.4.cloned.1.call-start
  8.1 0.7 all-gather.4.cloned.1.call-update
  8.7 0.0 reduce-scatter.5.cloned.1.call-start
  8.8 1.1 copy-done
  9.9 7.9 %bitcast_convert_fusion = bf16[4096,1024]{1,0:T(8,128)(2,1)} fusion(bf16[1,1,4,96,4096]{4,3,2,1,0:T(8,128)(2,1)S(1)} %copy-done, bf16[1,1,4,96,1024]{4,3,2,1,0:T(8,128)(2,1)} %param.11), kind=kOutput, calls=%fused_computation.2 | convolution fusion | flops 3225419776 | bytes 12320768 | tf_op jit(solution)/shard_map/dot_general | solution.py:59
  17.8 0.0 copy-start.2
  17.8 0.0 copy-start.3
  17.8 0.0 reduce-scatter.5.cloned.1.call-update
  17.8 0.0 reduce-scatter.3.cloned.1.call-start
  17.8 0.6 copy-done.2
  18.4 0.1 copy.21
  18.6 31.8 %all-gather = bf16[1,1,4,256]{2,1,0,3:T(2,128)(2,1)S(1)} all-gather(bf16[1,1,4,32]{2,1,0,3:T(2,128)(2,1)S(1)} %copy.21), channel_id=2, replica_groups=mesh['section'=4,'wide_0'=4,'wide_1'=2,'narrow_0'=2,'narrow_1'=2] {'wide..., dimensions={3}, use_global_device_ids=true | all-gather | bytes 2304 | tf_op jit(solution)/shard_map/all_gather | solution.py:44
  50.3 0.1 convert_element_type.58
  50.5 0.0 copy-done.3
  50.5 0.1 copy.22
  50.6 70.8 %all-gather.4.cloned.1.call-done = bf16[1,1,4,256,4096]{4,3,2,1,0:T(8,128)(2,1)} async-done(((bf16[1,1,4,32,4096]{4,3,2,1,0:T(8,128)(2,1)}), bf16[1,1,4,256,4096]{4,3,2,1,0:T(8,128)(2,1)}) %all-gather.4.cloned.1.call-update) | async-done | bytes 8388624 | tf_op jit(solution)/shard_map/all_gather | solution.py:43
  121.4 14.1 %fusion.5 = bf16[896,4096]{0,1:T(8,128)(2,1)} fusion(bf16[1,1,4,256,4096]{4,3,2,1,0:T(8,128)(2,1)} %all-gather.4.cloned.1.call-done, f32[4,256]{1,0:T(4,128)S(1)} %copy.22, bf16[1,1,4,256,896]{4,3,2,1,0:T(8,128)(2,1)} %param.12), kind=kOutput, calls=%fused_computation.7 | convolution fusion | flops 7532445696 | bytes 17567744 | tf_op jit(solution)/shard_map/dot_general | solution.py:52
  135.6 0.0 reduce-scatter.3.cloned.1.call-update
  135.6 17.6 %reduce-scatter.5.cloned.1.call-done = bf16[128,1024]{1,0:T(8,128)(2,1)} async-done(((bf16[4096,1024]{1,0:T(8,128)(2,1)}), bf16[128,1024]{1,0:T(8,128)(2,1)}) %reduce-scatter.5.cloned.1.call-update) | async-done | bytes 262160 | tf_op jit(solution)/shard_map/reduce_scatter | solution.py:58
  153.2 1.7 fusion.16
  154.9 72.7 %reduce-scatter.3.cloned.1.call-done = bf16[896,1024]{0,1:T(8,128)(2,1)} async-done(((bf16[896,4096]{0,1:T(8,128)(2,1)}), bf16[896,1024]{0,1:T(8,128)(2,1)}) %reduce-scatter.3.cloned.1.call-update) | async-done | bytes 1835024 | tf_op jit(solution)/shard_map/reduce_scatter | solution.py:55
  227.6 3.0 %fusion.8 = f32[]{:T(128)} fusion(bf16[896,1024]{0,1:T(8,128)(2,1)} %reduce-scatter.3.cloned.1.call-done), kind=kLoop, calls=%fused_computation.10 | loop fusion | flops 2752511 | bytes 1835012 | tf_op jit(solution)/shard_map/reduce_sum | solution.py:66
  231.9 9.0 %psum.35 = f32[]{:T(128)} all-reduce(f32[]{:T(128)S(6)} %add.26), channel_id=1, replica_groups=mesh['section'=4,'wide_0'=4,'wide_1'=2,'narrow_0'=2,'narrow_1'=2] {'sect..., use_global_device_ids=true, to_apply=%region_4.5 | all-reduce | flops 1 | bytes 8 | tf_op jit(solution)/shard_map/psum | solution.py:21
  240.9 9.3 %psum.36 = f32[]{:T(128)} all-reduce(f32[]{:T(128)} %psum.35), channel_id=1, replica_groups=mesh['section'=4,'wide_0'=4,'wide_1'=2,'narrow_0'=2,'narrow_1'=2] {'wide..., use_global_device_ids=true, to_apply=%region_5.6 | all-reduce | flops 1 | bytes 8 | tf_op jit(solution)/shard_map/psum | solution.py:21
  250.2 5.9 %psum.37 = f32[]{:T(128)} all-reduce(f32[]{:T(128)} %psum.36), channel_id=1, replica_groups=mesh['section'=4,'wide_0'=4,'wide_1'=2,'narrow_0'=2,'narrow_1'=2] {'wide..., use_global_device_ids=true, to_apply=%region_6.7 | all-reduce | flops 1 | bytes 8 | tf_op jit(solution)/shard_map/psum | solution.py:21
  256.0 5.0 %copy.20 = f32[1,896,1024]{1,2,0:T(8,128)} copy(f32[1,896,1024]{2,1,0:T(8,128)} %param.17) | data formatting | bytes 7340032 | tf_op args[7]
  261.1 4.4 %psum.38 = f32[]{:T(128)} all-reduce(f32[]{:T(128)} %psum.37), channel_id=1, replica_groups=mesh['section'=4,'wide_0'=4,'wide_1'=2,'narrow_0'=2,'narrow_1'=2] {'narr..., use_global_device_ids=true, to_apply=%region_7.8 | all-reduce | flops 1 | bytes 8 | tf_op jit(solution)/shard_map/psum | solution.py:21
  265.4 3.8 %copy.19 = bf16[1,896,1024]{1,2,0:T(8,128)(2,1)} copy(bf16[1,896,1024]{2,1,0:T(8,128)(2,1)} %param.16) | data formatting | bytes 3670016 | tf_op args[6]
  269.2 9.4 %psum.39 = f32[]{:T(128)} all-reduce(f32[]{:T(128)} %psum.38), channel_id=1, replica_groups=mesh['section'=4,'wide_0'=4,'wide_1'=2,'narrow_0'=2,'narrow_1'=2] {'narr..., use_global_device_ids=true, to_apply=%region_8.9 | all-reduce | flops 1 | bytes 8 | tf_op jit(solution)/shard_map/psum | solution.py:21
  279.3 6.5 %fusion.12 = (f32[1,896,1024]{1,2,0:T(8,128)}, bf16[1,896,1024]{1,2,0:T(8,128)(2,1)}) fusion(bf16[896,1024]{0,1:T(8,128)(2,1)} %reduce-scatter.3.cloned.1.call-done, f32[1,896,1024]{1,2,0:T(8,128)} %copy.20, f32[]{:T(128)S(6)} %min_shard_map.3, bf16[1,896,1024]{1,2,0:T(8,128)(2,1)} %copy.19), kind=kLoop, calls=%fused_computation.15 | loop fusion | flops 7340032 | bytes 12845060 | tf_op jit(solution)/shard_map/broadcast_in_dim | solution.py:78
  285.8 3.8 %copy.24 = bf16[1,896,1024]{2,1,0:T(8,128)(2,1)} copy(bf16[1,896,1024]{1,2,0:T(8,128)(2,1)} %get-tuple-element.13) | data formatting | bytes 3670016
  289.6 0.0 copy-start.1
  289.6 5.0 %copy.25 = f32[1,896,1024]{2,1,0:T(8,128)} copy(f32[1,896,1024]{1,2,0:T(8,128)} %get-tuple-element.12) | data formatting | bytes 7340032
  294.6 0.0 copy-done.1
  294.6 2.1 fusion.19
  (1 shorter events, 0.0 us)
Async XLA Ops:
  8.0 1.9 copy-start
  8.0 113.4 %all-gather.4.cloned.1.call-start = ((), (), s32[]{:S(2)}) async-start(), calls=%async_computation.4 | async-start | bytes 9437184 | tf_op jit(solution)/shard_map/all_gather | solution.py:43
  8.7 144.4 %reduce-scatter.5.cloned.1.call-start = ((), (), s32[]{:S(2)}) async-start(), calls=%async_computation.3 | async-start | bytes 8650752 | tf_op jit(solution)/shard_map/reduce_scatter | solution.py:58
  17.8 0.7 copy-start.2
  17.8 32.7 %copy-start.3 = (s32[1,1,4]{2,1,0:T(1,128)S(1)}, s32[1,1,4]{2,1,0:T(1,128)}, u32[]{:S(2)}) copy-start(s32[1,1,4]{2,1,0:T(1,128)} %param.15) | copy-start | bytes 52
  17.8 209.8 %reduce-scatter.3.cloned.1.call-start = ((), (), s32[]{:S(2)}) async-start(), calls=%async_computation.2 | async-start | bytes 9175040 | tf_op jit(solution)/shard_map/reduce_scatter | solution.py:55
  289.6 5.0 %copy-start.1 = (bf16[128,1024]{1,0:T(8,128)(2,1)S(1)}, bf16[128,1024]{1,0:T(8,128)(2,1)}, u32[]{:S(2)}) copy-start(bf16[128,1024]{1,0:T(8,128)(2,1)} %reduce-scatter.5.cloned.1.call-done) | copy-start | bytes 786436
Sparse Core Ops, SparseCore 0:
  11.1 110.2 all-gather.3
Sparse Core Ops, SparseCore 1:
  17.9 135.2 reduce-scatter.4
  155.4 72.1 reduce-scatter.2
where the time goes:
time: 305 us; the launch traced here: 304 us
  waiting for transfers between devices  162 us (53%)
  blocking collectives  69.7 us (23%)
  matrix products  22 us (7%)
  local copies, waits for them, and re-layouts  19.5 us (6%)
  between operations  17.5 us (6%)
  other arithmetic  13.5 us (4%)
    reduce_scatter x1, waiting for transfers between devices, on_device(): lax.psum_scatter(summed.astype(jnp.bfloat16), NARROW, scatter_dimension=1...  72.7 us
    all_gather x1, waiting for transfers between devices, on_device(): cot_piece = lax.all_gather(cotangent, WIDE, axis=1, tiled=True)  70.8 us
    psum x5, blocking collectives, over_axes(): shard = lax.psum(shard, axis)  37.9 us
    all_gather x1, blocking collectives, on_device(): gate_piece = lax.all_gather(gate_local, WIDE, axis=1, tiled=True)  31.8 us
    unnamed x13, local copies, waits for them, and re-layouts  19.4 us
    reduce_scatter x1, waiting for transfers between devices, on_device(): lax.psum_scatter(lax.dot_general(input_rows, value_cot_rows, (((0,), (0,)...  17.6 us
    dot_general x1, matrix products, on_device(): lax.dot_general(hidden_local, scaled, (((0, 1), (0, 1)), ((), ())), prefe...  14.1 us
    dot_general x1, matrix products, on_device(): lax.dot_general(input_rows, value_cot_rows, (((0,), (0,)), ((), ())), pre...  7.87 us
  transfers between devices with their start and end apart: 3, of which 3 were waited for; matrix products, arithmetic and copies ran while one was open for 8% of the time, Pallas kernels for 0%

commit v1 on v0

--- a/solution.py
+++ b/solution.py
@@ -40,7 +40,7 @@
     cotangent = expert_cotangent[0, 0]
     gate_local = slot_gate[0, 0]
     live_count = slot_count[0, 0]
-    cot_piece = lax.all_gather(cotangent, WIDE, axis=1, tiled=True)
+    cot_piece = jnp.concatenate(lax.all_gather(cotangent, WIDE), axis=1)
     gate_piece = lax.all_gather(gate_local, WIDE, axis=1, tiled=True)
     length = cot_piece.shape[1]
     positions = jnp.arange(length, dtype=jnp.int32)

time: 305 us -> 305 us (level)
  other arithmetic: 13.5 us -> 23.6 us
  waiting for transfers between devices: 162 us -> 152 us
    convert_element_type x0 -> x1, other arithmetic: none -> 10.1 us  [on_device(): (coefficient[:, :, None] * cot_piece.astype(jnp.float32)).astype(jnp.bflo...]
    reduce_scatter x1, waiting for transfers between devices: 17.6 us -> 7.71 us  [on_device(): lax.psum_scatter(lax.dot_general(input_rows, value_cot_rows, (((0,), (0,)...]
  transfers between devices with their start and end apart: 3 -> 3, of which waited for: 3 -> 3; matrix products, arithmetic and copies ran while one was open for 8% -> 11% of each run, Pallas kernels for 0% -> 0%
where the time goes in v1:
time: 305 us; the launch traced here: 304 us
  waiting for transfers between devices  152 us (50%)
  blocking collectives  69.7 us (23%)
  other arithmetic  23.6 us (8%)
  matrix products  21.8 us (7%)
  local copies, waits for them, and re-layouts  19.5 us (6%)
  between operations  17.5 us (6%)
    reduce_scatter x1, waiting for transfers between devices, on_device(): lax.psum_scatter(summed.astype(jnp.bfloat16), NARROW, scatter_dimension=1...  72.7 us
    all_gather x1, waiting for transfers between devices, on_device(): cot_piece = jnp.concatenate(lax.all_gather(cotangent, WIDE), axis=1)  70.8 us
    psum x5, blocking collectives, over_axes(): shard = lax.psum(shard, axis)  37.9 us
    all_gather x1, blocking collectives, on_device(): gate_piece = lax.all_gather(gate_local, WIDE, axis=1, tiled=True)  31.8 us
    unnamed x13, local copies, waits for them, and re-layouts  19.4 us
    dot_general x1, matrix products, on_device(): lax.dot_general(hidden_local, scaled, (((0, 1), (0, 1)), ((), ())), prefe...  13.9 us
    convert_element_type x1, other arithmetic, on_device(): (coefficient[:, :, None] * cot_piece.astype(jnp.float32)).astype(jnp.bflo...  10.1 us
    dot_general x1, matrix products, on_device(): lax.dot_general(input_rows, value_cot_rows, (((0,), (0,)), ((), ())), pre...  7.87 us
  transfers between devices with their start and end apart: 3, of which 3 were waited for; matrix products, arithmetic and copies ran while one was open for 11% of the time, Pallas kernels for 0%

profile of v1, /device:TPU:1, one launch (start us, length us, event | category | flops | bytes accessed | tf_op | source)
XLA Modules:
  0.0 304.2 jit_solution(6058906786890718244)
XLA Ops:
  8.0 0.0 copy-start
  8.0 0.0 all-gather.4.cloned.1.call-start
  8.1 0.7 all-gather.4.cloned.1.call-update
  8.7 0.0 reduce-scatter.5.cloned.1.call-start
  8.8 1.1 copy-done
  9.9 7.9 %bitcast_convert_fusion = bf16[4096,1024]{1,0:T(8,128)(2,1)} fusion(bf16[1,1,4,96,4096]{4,3,2,1,0:T(8,128)(2,1)S(1)} %copy-done, bf16[1,1,4,96,1024]{4,3,2,1,0:T(8,128)(2,1)} %param.11), kind=kOutput, calls=%fused_computation.3 | convolution fusion | flops 3225419776 | bytes 12320768 | tf_op jit(solution)/shard_map/dot_general | solution.py:59
  17.8 0.0 copy-start.2
  17.8 0.0 copy-start.3
  17.8 0.0 reduce-scatter.5.cloned.1.call-update
  17.8 0.0 reduce-scatter.3.cloned.1.call-start
  17.8 0.6 copy-done.2
  18.4 0.1 copy.27
  18.6 31.8 %all-gather = bf16[1,1,4,256]{2,1,0,3:T(2,128)(2,1)S(1)} all-gather(bf16[1,1,4,32]{2,1,0,3:T(2,128)(2,1)S(1)} %copy.27), channel_id=2, replica_groups=mesh['section'=4,'wide_0'=4,'wide_1'=2,'narrow_0'=2,'narrow_1'=2] {'wide..., dimensions={3}, use_global_device_ids=true | all-gather | bytes 2304 | tf_op jit(solution)/shard_map/all_gather | solution.py:44
  50.3 0.1 convert_element_type.68
  50.5 0.0 copy-done.3
  50.5 0.1 copy.28
  50.6 70.8 %all-gather.4.cloned.1.call-done = bf16[8,1,4,32,4096]{4,3,0,2,1:T(8,128)(2,1)} async-done(((bf16[1,1,4,32,4096]{4,3,0,2,1:T(8,128)(2,1)}), bf16[8,1,4,32,4096]{4,3,0,2,1:T(8,128)(2,1)}) %all-gather.4.cloned.1.call-update) | async-done | bytes 8388624 | tf_op jit(solution)/shard_map/all_gather | solution.py:43
  121.4 10.1 %fusion.1 = bf16[4,8,32,4096]{3,2,1,0:T(8,128)(2,1)} fusion(bf16[8,1,4,32,4096]{4,3,0,2,1:T(8,128)(2,1)} %all-gather.4.cloned.1.call-done, f32[4,8,32]{2,1,0:T(8,128)S(1)} %copy.28), kind=kLoop, calls=%fused_computation.2 | loop fusion | flops 12582912 | bytes 16781312 | tf_op jit(solution)/shard_map/convert_element_type | solution.py:51
  131.5 13.9 %fusion.2 = bf16[896,4096]{0,1:T(8,128)(2,1)} fusion(bf16[4,256,4096]{2,1,0:T(8,128)(2,1)} %bitcast.62, bf16[1,1,4,256,896]{4,3,2,1,0:T(8,128)(2,1)} %param.12), kind=kOutput, calls=%fused_computation.5 | convolution fusion | flops 7519862784 | bytes 17563648 | tf_op jit(solution)/shard_map/dot_general | solution.py:52
  145.4 0.0 reduce-scatter.3.cloned.1.call-update
  145.5 7.7 %reduce-scatter.5.cloned.1.call-done = bf16[128,1024]{1,0:T(8,128)(2,1)} async-done(((bf16[4096,1024]{1,0:T(8,128)(2,1)}), bf16[128,1024]{1,0:T(8,128)(2,1)}) %reduce-scatter.5.cloned.1.call-update) | async-done | bytes 262160 | tf_op jit(solution)/shard_map/reduce_scatter | solution.py:58
  153.2 1.7 fusion.11
  154.9 72.7 %reduce-scatter.3.cloned.1.call-done = bf16[896,1024]{0,1:T(8,128)(2,1)} async-done(((bf16[896,4096]{0,1:T(8,128)(2,1)}), bf16[896,1024]{0,1:T(8,128)(2,1)}) %reduce-scatter.3.cloned.1.call-update) | async-done | bytes 1835024 | tf_op jit(solution)/shard_map/reduce_scatter | solution.py:55
  227.6 3.0 %fusion.3 = f32[]{:T(128)} fusion(bf16[896,1024]{0,1:T(8,128)(2,1)} %reduce-scatter.3.cloned.1.call-done), kind=kLoop, calls=%fused_computation.8 | loop fusion | flops 2752511 | bytes 1835012 | tf_op jit(solution)/shard_map/reduce_sum | solution.py:66
  231.9 9.0 %psum.35 = f32[]{:T(128)} all-reduce(f32[]{:T(128)S(6)} %add.26), channel_id=1, replica_groups=mesh['section'=4,'wide_0'=4,'wide_1'=2,'narrow_0'=2,'narrow_1'=2] {'sect..., use_global_device_ids=true, to_apply=%region_4.5 | all-reduce | flops 1 | bytes 8 | tf_op jit(solution)/shard_map/psum | solution.py:21
  240.9 9.3 %psum.36 = f32[]{:T(128)} all-reduce(f32[]{:T(128)} %psum.35), channel_id=1, replica_groups=mesh['section'=4,'wide_0'=4,'wide_1'=2,'narrow_0'=2,'narrow_1'=2] {'wide..., use_global_device_ids=true, to_apply=%region_5.6 | all-reduce | flops 1 | bytes 8 | tf_op jit(solution)/shard_map/psum | solution.py:21
  250.2 5.9 %psum.37 = f32[]{:T(128)} all-reduce(f32[]{:T(128)} %psum.36), channel_id=1, replica_groups=mesh['section'=4,'wide_0'=4,'wide_1'=2,'narrow_0'=2,'narrow_1'=2] {'wide..., use_global_device_ids=true, to_apply=%region_6.7 | all-reduce | flops 1 | bytes 8 | tf_op jit(solution)/shard_map/psum | solution.py:21
  256.0 3.8 %copy.25 = bf16[1,896,1024]{1,2,0:T(8,128)(2,1)} copy(bf16[1,896,1024]{2,1,0:T(8,128)(2,1)} %param.16) | data formatting | bytes 3670016 | tf_op args[6]
  259.8 4.4 %psum.38 = f32[]{:T(128)} all-reduce(f32[]{:T(128)} %psum.37), channel_id=1, replica_groups=mesh['section'=4,'wide_0'=4,'wide_1'=2,'narrow_0'=2,'narrow_1'=2] {'narr..., use_global_device_ids=true, to_apply=%region_7.8 | all-reduce | flops 1 | bytes 8 | tf_op jit(solution)/shard_map/psum | solution.py:21
  264.2 5.0 %copy.26 = f32[1,896,1024]{1,2,0:T(8,128)} copy(f32[1,896,1024]{2,1,0:T(8,128)} %param.17) | data formatting | bytes 7340032 | tf_op args[7]
  269.2 9.4 %psum.39 = f32[]{:T(128)} all-reduce(f32[]{:T(128)} %psum.38), channel_id=1, replica_groups=mesh['section'=4,'wide_0'=4,'wide_1'=2,'narrow_0'=2,'narrow_1'=2] {'narr..., use_global_device_ids=true, to_apply=%region_8.9 | all-reduce | flops 1 | bytes 8 | tf_op jit(solution)/shard_map/psum | solution.py:21
  279.3 6.5 %fusion.7 = (f32[1,896,1024]{1,2,0:T(8,128)}, bf16[1,896,1024]{1,2,0:T(8,128)(2,1)}) fusion(bf16[896,1024]{0,1:T(8,128)(2,1)} %reduce-scatter.3.cloned.1.call-done, f32[1,896,1024]{1,2,0:T(8,128)} %copy.26, f32[]{:T(128)S(6)} %min_shard_map.3, bf16[1,896,1024]{1,2,0:T(8,128)(2,1)} %copy.25), kind=kLoop, calls=%fused_computation.13 | loop fusion | flops 7340032 | bytes 12845060 | tf_op jit(solution)/shard_map/broadcast_in_dim | solution.py:78
  285.8 5.0 %copy.32 = f32[1,896,1024]{2,1,0:T(8,128)} copy(f32[1,896,1024]{1,2,0:T(8,128)} %get-tuple-element.16) | data formatting | bytes 7340032
  290.8 0.0 copy-start.1
  290.8 3.8 %copy.31 = bf16[1,896,1024]{2,1,0:T(8,128)(2,1)} copy(bf16[1,896,1024]{1,2,0:T(8,128)(2,1)} %get-tuple-element.17) | data formatting | bytes 3670016
  294.6 0.0 copy-done.1
  294.6 2.1 fusion.14
  (1 shorter events, 0.0 us)
Async XLA Ops:
  8.0 1.9 copy-start
  8.0 113.4 %all-gather.4.cloned.1.call-start = ((), (), s32[]{:S(2)}) async-start(), calls=%async_computation.4 | async-start | bytes 9437184 | tf_op jit(solution)/shard_map/all_gather | solution.py:43
  8.7 144.4 %reduce-scatter.5.cloned.1.call-start = ((), (), s32[]{:S(2)}) async-start(), calls=%async_computation.3 | async-start | bytes 8650752 | tf_op jit(solution)/shard_map/reduce_scatter | solution.py:58
  17.8 0.7 copy-start.2
  17.8 32.7 %copy-start.3 = (s32[1,1,4]{2,1,0:T(1,128)S(1)}, s32[1,1,4]{2,1,0:T(1,128)}, u32[]{:S(2)}) copy-start(s32[1,1,4]{2,1,0:T(1,128)} %param.15) | copy-start | bytes 52
  17.8 209.8 %reduce-scatter.3.cloned.1.call-start = ((), (), s32[]{:S(2)}) async-start(), calls=%async_computation.2 | async-start | bytes 9175040 | tf_op jit(solution)/shard_map/reduce_scatter | solution.py:55
  290.8 3.8 %copy-start.1 = (bf16[128,1024]{1,0:T(8,128)(2,1)S(1)}, bf16[128,1024]{1,0:T(8,128)(2,1)}, u32[]{:S(2)}) copy-start(bf16[128,1024]{1,0:T(8,128)(2,1)} %reduce-scatter.5.cloned.1.call-done) | copy-start | bytes 786436
Sparse Core Ops, SparseCore 0:
  11.1 110.2 all-gather.3
Sparse Core Ops, SparseCore 1:
  17.9 135.2 reduce-scatter.4
  155.4 72.1 reduce-scatter.2
